TPU v7x, 32 devices: a whole 2x2x4 slice. The times are simulated.
32 devices in a mesh: group: 4 (over z), seq: 4 (over y, core), mp: 2 (over x).
Axes of the slice: x: 2, y: 2, z: 4, core: 2. Of those that a mesh axis runs over, the one named last changes fastest.
Arguments:
- patches: bfloat16 [8192, 640], P(('group', 'seq')), may hold values from -6 to 6
- w_merge1: bfloat16 [4, 640, 2560], P(None, 'seq', 'mp'), may hold values from -0.125 to 0.125
- w_merge2: bfloat16 [2560, 4096], P('mp', 'seq'), may hold values from -0.125 to 0.125
- w_query: bfloat16 [4096, 4096], P('seq', 'mp'), may hold values from -0.09375 to 0.09375
- w_keyval: bfloat16 [4096, 2, 1024], P('seq', None, 'mp'), may hold values from -0.09375 to 0.09375
- attn_grad: bfloat16 [2048, 4096], P(('group', 'seq'), 'mp'), may hold values from -6 to 6
- sample_ids: int32 [4, 512], P('group'), may hold values from 0 to 7, never falling along the last dimension, each value on 1 to 384 neighbouring positions
Outputs:
- patch_grad: bfloat16 [8192, 640], P(('group', 'seq', 'mp'))
Inputs may be any that keep to these rules, and one draw needn't show every extreme that they name: `sample_ids`: in each sequence never falls; every sample spans 1 to 384 tokens.
All inputs are finite; a program needn't handle non-finite values.
Results may differ from a plain program's by a relative error of at most 0.035.
Values may be sent and summed in bfloat16 or wider, within the bound.
No kernel may reach another device: no remote copies, remote signals or barrier semaphores. Data moves between devices by JAX's collectives and lax.ppermute only.
A program may use at most 128 MiB of HBM per device.

v0:
```python
import jax
import jax.numpy as jnp
from jax import lax
from jax.sharding import PartitionSpec as P

HEAD = 128
EPSILON = 1e-06
NEGATIVE = 1e30


def shifted_2(value, axis, steps):
    count = lax.axis_size(axis)
    initial, last = (max(0, -steps), min(count, count - steps))
    return lax.ppermute(value, axis, [(source, source + steps) for source in range(initial, last)])


def gelu_grad(inputs):
    normal_cdf = 0.5 * (1.0 + lax.erf(inputs * 0.7071067811865476))
    normal_pdf = jnp.exp(-0.5 * inputs * inputs) * 0.3989422804014327
    return normal_cdf + inputs * normal_pdf


def fetch_earlier(own_keyval, offset):
    return shifted_2(own_keyval, "seq", offset)


def return_terms(terms, offset):
    return (
        shifted_2(terms[0].astype(jnp.bfloat16), "seq", -offset).astype(jnp.float32),
        shifted_2(terms[1].astype(jnp.bfloat16), "seq", -offset).astype(jnp.float32),
    )


def local(patches, w_merge1, w_merge2, w_query, w_keyval, attn_grad, sample_ids):
    patch_rows, feat_width = patches.shape
    tok_rows = patch_rows // 4
    score_scale = HEAD ** (-0.5)
    values = patches.astype(jnp.float32)
    row_mean = jnp.mean(values, -1, keepdims=True)
    ln_scale = lax.rsqrt(
        jnp.mean(values * values, -1, keepdims=True) - row_mean * row_mean + EPSILON
    )
    normed = (values - row_mean) * ln_scale
    merge_in = normed.astype(jnp.bfloat16).reshape(tok_rows, 4 * feat_width)
    first_tile = lax.all_gather(w_merge1, "seq", axis=1, tiled=True)
    first_flat = first_tile.reshape(4 * feat_width, first_tile.shape[2])
    hidden_pre = jnp.dot(merge_in, first_flat, preferred_element_type=jnp.float32)
    hidden = jax.nn.gelu(hidden_pre, approximate=False).astype(jnp.bfloat16)
    second_tile = lax.all_gather(w_merge2, "seq", axis=1, tiled=True)
    model_width = second_tile.shape[1]
    partial_value = jnp.dot(hidden, second_tile, preferred_element_type=jnp.float32)
    merged = lax.psum(partial_value.astype(jnp.bfloat16), "mp")
    merged_f = merged.astype(jnp.float32)
    rms_scale = lax.rsqrt(jnp.mean(merged_f * merged_f, -1, keepdims=True) + EPSILON)
    normed_tok = merged_f * rms_scale
    query_tile, keyval_tile = (
        lax.all_gather(w_query, "seq", axis=0, tiled=True),
        lax.all_gather(w_keyval, "seq", axis=0, tiled=True),
    )
    kv_part = keyval_tile.shape[2]
    keyval_flat = keyval_tile.reshape(model_width, 2 * kv_part)
    normed_bf = normed_tok.astype(jnp.bfloat16)
    queries = jnp.dot(normed_bf, query_tile, preferred_element_type=jnp.float32).astype(
        jnp.bfloat16
    )
    own_keyval = jnp.dot(normed_bf, keyval_flat, preferred_element_type=jnp.float32).astype(
        jnp.bfloat16
    )
    query_part = queries.shape[1]
    kv_local = kv_part // HEAD
    per_kv = query_part // HEAD // kv_local
    run_ids = sample_ids[0]
    run_len = run_ids.shape[0]
    own_start = lax.axis_index("seq") * tok_rows
    reach = min(lax.axis_size("seq") - 1, (run_len // 2 + 2 * tok_rows - 2) // tok_rows)
    pieces = [own_keyval]
    for offset in range(1, reach + 1):
        pieces.insert(0, fetch_earlier(own_keyval, offset))
    window_kv = jnp.concatenate(pieces, 0)
    window_rows = window_kv.shape[0]
    key_pos = own_start - reach * tok_rows + jnp.arange(window_rows, dtype=jnp.int32)
    padded_ids = jnp.concatenate([jnp.full((reach * tok_rows,), -1, jnp.int32), run_ids], 0)
    key_ids = lax.dynamic_slice_in_dim(padded_ids, own_start, window_rows, 0)
    total_rows = window_kv.shape[0]
    key_heads = window_kv[:, :kv_part].reshape(total_rows, kv_local, HEAD)
    value_heads = window_kv[:, kv_part:].reshape(total_rows, kv_local, HEAD)
    query_pos = own_start + jnp.arange(tok_rows, dtype=jnp.int32)
    own_ids = lax.dynamic_slice_in_dim(run_ids, own_start, tok_rows, 0)
    allowed = (query_pos[:, None] >= key_pos[None, :]) & (own_ids[:, None] == key_ids[None, :])
    query_heads = queries.reshape(tok_rows, kv_local, per_kv, HEAD)
    scores = (
        jnp.einsum("tkgd,ukd->kgtu", query_heads, key_heads, preferred_element_type=jnp.float32)
        * score_scale
    )
    scores = jnp.where(allowed, scores, -NEGATIVE)
    row_max = jnp.max(scores, -1, keepdims=True)
    shifted = jnp.exp(scores - row_max)
    soft = shifted / jnp.sum(shifted, -1, keepdims=True)
    soft_bf = soft.astype(jnp.bfloat16)
    attended = jnp.einsum(
        "kgtu,ukd->tkgd", soft_bf, value_heads, preferred_element_type=jnp.float32
    )
    grad_heads = attn_grad.reshape(tok_rows, kv_local, per_kv, HEAD)
    row_delta = jnp.sum(grad_heads.astype(jnp.float32) * attended, -1)
    dprob = jnp.einsum(
        "tkgd,ukd->kgtu", grad_heads, value_heads, preferred_element_type=jnp.float32
    )
    dscore = (soft * (dprob - jnp.transpose(row_delta, (1, 2, 0))[..., None])).astype(jnp.bfloat16)
    dquery = (
        jnp.einsum("kgtu,ukd->tkgd", dscore, key_heads, preferred_element_type=jnp.float32)
        * score_scale
    )
    dquery = dquery.astype(jnp.bfloat16).reshape(tok_rows, query_part)
    dkey_terms = (
        jnp.einsum("kgtu,tkgd->ukd", dscore, query_heads, preferred_element_type=jnp.float32)
        * score_scale
    )
    dvalue_terms = jnp.einsum(
        "kgtu,tkgd->ukd", soft_bf, grad_heads, preferred_element_type=jnp.float32
    )
    dkey = dkey_terms[reach * tok_rows :]
    dvalue = dvalue_terms[reach * tok_rows :]
    for offset in range(1, reach + 1):
        begin_row = (reach - offset) * tok_rows
        key_back, value_back = return_terms(
            (
                dkey_terms[begin_row : begin_row + tok_rows],
                dvalue_terms[begin_row : begin_row + tok_rows],
            ),
            offset,
        )
        dkey = dkey + key_back
        dvalue = dvalue + value_back
    grads_kv = jnp.concatenate(
        [
            dkey.astype(jnp.bfloat16).reshape(tok_rows, kv_part),
            dvalue.astype(jnp.bfloat16).reshape(tok_rows, kv_part),
        ],
        1,
    )
    dnormed_part = jnp.einsum("tc,dc->td", dquery, query_tile, preferred_element_type=jnp.float32)
    dnormed_part = dnormed_part + jnp.einsum(
        "tc,dc->td", grads_kv, keyval_flat, preferred_element_type=jnp.float32
    )
    dnormed = lax.psum(dnormed_part.astype(jnp.bfloat16), "mp").astype(jnp.float32)
    inner_mean = jnp.mean(dnormed * normed_tok, -1, keepdims=True)
    dmerged = (rms_scale * (dnormed - normed_tok * inner_mean)).astype(jnp.bfloat16)
    dhidden = jnp.einsum("td,hd->th", dmerged, second_tile, preferred_element_type=jnp.float32)
    dhidden_pre = (dhidden * gelu_grad(hidden_pre)).astype(jnp.bfloat16)
    dmerge_part = jnp.einsum(
        "th,fh->tf", dhidden_pre, first_flat, preferred_element_type=jnp.float32
    )
    dmerge_in = lax.psum_scatter(
        dmerge_part.reshape(patch_rows, feat_width).astype(jnp.bfloat16),
        "mp",
        scatter_dimension=0,
        tiled=True,
    ).astype(jnp.float32)
    share_rows = dmerge_in.shape[0]
    begin = lax.axis_index("mp") * share_rows
    own_normed = lax.dynamic_slice_in_dim(normed, begin, share_rows, 0)
    own_scale = lax.dynamic_slice_in_dim(ln_scale, begin, share_rows, 0)
    first_mean = jnp.mean(dmerge_in, -1, keepdims=True)
    second_mean = jnp.mean(dmerge_in * own_normed, -1, keepdims=True)
    patch_grad = own_scale * (dmerge_in - first_mean - own_normed * second_mean)
    return patch_grad.astype(jnp.bfloat16)


def solution(mesh):
    in_specs = (
        P(("group", "seq"), None),
        P(None, "seq", "mp"),
        P("mp", "seq"),
        P("seq", "mp"),
        P("seq", None, "mp"),
        P(("group", "seq"), "mp"),
        P("group", None),
    )
    out_specs = P(("group", "seq", "mp"), None)
    return jax.shard_map(local, mesh=mesh, in_specs=in_specs, out_specs=out_specs, check_vma=False)
```

profile of v0, /device:TPU:0, one launch (start us, length us, event | category | flops | bytes accessed | tf_op | source)
XLA Modules:
  0.0 488.3 jit_solution(8009914416394618098)
XLA Ops:
  6.5 0.7 all-gather.5.cloned.1.call-update
  7.3 0.7 all-gather.7.cloned.1.call-update
  8.1 0.7 all-gather.9.cloned.1.call-update
  8.8 0.3 convert_reduce_fusion
  9.1 1.4 fusion.20
  10.4 0.4 reshape.109
  10.8 48.7 %all-gather.5.cloned.1.call-done = bf16[4,640,1280]{2,1,0:T(8,128)(2,1)} async-done(((bf16[4,160,1280]{2,1,0:T(8,128)(2,1)}), bf16[4,640,1280]{2,1,0:T(8,128)(2,1)}) %all-gather.5.cloned.1.call-update) | async-done | bytes 6553616 | tf_op jit(solution)/shard_map/all_gather | solution.py:45
  59.5 3.9 fusion.140
  63.4 67.9 %all-gather.7.cloned.1.call-done = bf16[1280,4096]{1,0:T(8,128)(2,1)} async-done(((bf16[1280,1024]{1,0:T(8,128)(2,1)}), bf16[1280,4096]{1,0:T(8,128)(2,1)}) %all-gather.7.cloned.1.call-update) | async-done | bytes 10485776 | tf_op jit(solution)/shard_map/all_gather | solution.py:49
  131.3 7.8 %convolution_convert_fusion = bf16[128,4096]{1,0:T(8,128)(2,1)} fusion(bf16[1280,4096]{1,0:T(8,128)(2,1)} %all-gather.7.cloned.1.call-done, f32[128,1280]{1,0:T(8,128)S(1)} %fusion.140), kind=kOutput, calls=%fused_computation.3 | convolution fusion | flops 1353351168 | bytes 12189696 | tf_op jit(solution)/shard_map/dot_general | solution.py:51
  139.1 0.0 all-gather.11.cloned.1.call-start
  139.1 0.5 all-gather.11.cloned.1.call-update
  139.8 0.1 pad_dynamic-slice_fusion
  139.9 51.3 %all-gather.9.cloned.1.call-done = bf16[4096,2,512]{2,1,0:T(2,128)(2,1)} async-done(((bf16[1024,2,512]{2,1,0:T(2,128)(2,1)}), bf16[4096,2,512]{2,1,0:T(2,128)(2,1)}) %all-gather.9.cloned.1.call-update) | async-done | bytes 8388624 | tf_op jit(solution)/shard_map/all_gather | solution.py:58
  191.1 9.3 %copy.52 = bf16[512,8,2,512]{3,1,2,0:T(8,128)(2,1)} copy(bf16[512,8,2,512]{3,2,1,0:T(2,128)(2,1)} %bitcast.81) | data formatting | bytes 16777216
  200.5 33.0 %all-reduce.4.cloned.1.call-done = bf16[128,4096]{1,0:T(8,128)(2,1)} async-done(((bf16[128,4096]{1,0:T(8,128)(2,1)}), bf16[128,4096]{1,0:T(8,128)(2,1)}) %all-reduce.4.cloned.1.call-update) | async-done | bytes 1048592 | tf_op jit(solution)/shard_map/psum | solution.py:52
  233.5 1.5 fusion.8
  235.0 5.1 %convolution_convert_fusion.3 = bf16[128,1024]{1,0:T(8,128)(2,1)S(1)} fusion(bf16[4096,1024]{1,0:T(8,128)(2,1)} %bitcast.79, bf16[128,4096]{1,0:T(8,128)(2,1)} %all-reduce.4.cloned.1.call-done, f32[128]{0:T(128)S(1)} %add_rsqrt_fusion.1), kind=kOutput, calls=%fused_computation.43 | convolution fusion | flops 1075445760 | bytes 9699840 | tf_op jit(solution)/shard_map/dot_general | solution.py:66
  240.1 1.6 collective-permute-start.2
  241.7 3.7 collective-permute-start.1
  245.4 1.5 collective-permute-start
  246.9 0.3 copy.22
  247.2 0.2 compare_and_fusion
  247.4 10.1 %collective-permute-done.1 = bf16[128,1024]{1,0:T(8,128)(2,1)S(1)} collective-permute-done((bf16[128,1024]{1,0:T(8,128)(2,1)S(1)}, bf16[128,1024]{1,0:T(8,128)(2,1)S(1)}, u32[]{:S(2)}, u32[]{:S(2)}) %collective-permute-start.1) | collective-permute-done | bytes 262176 | tf_op jit(solution)/shard_map/ppermute | solution.py:14
  257.5 8.7 %collective-permute-done = bf16[128,1024]{1,0:T(8,128)(2,1)S(1)} collective-permute-done((bf16[128,1024]{1,0:T(8,128)(2,1)S(1)}, bf16[128,1024]{1,0:T(8,128)(2,1)S(1)}, u32[]{:S(2)}, u32[]{:S(2)}) %collective-permute-start) | collective-permute-done | bytes 262176 | tf_op jit(solution)/shard_map/ppermute | solution.py:14
  266.2 0.1 pad_maximum_fusion
  266.3 0.1 fusion.134
  266.4 0.1 reshape.114
  266.5 0.3 copy.35
  266.9 0.1 reshape.112
  267.0 0.3 copy.37
  267.3 77.9 %all-gather.11.cloned.1.call-done = bf16[4096,2048]{1,0:T(8,128)(2,1)} async-done(((bf16[1024,2048]{1,0:T(8,128)(2,1)}), bf16[4096,2048]{1,0:T(8,128)(2,1)}) %all-gather.11.cloned.1.call-update) | async-done | bytes 16777232 | tf_op jit(solution)/shard_map/all_gather | solution.py:57
  345.2 8.2 %convolution_convert_fusion.2 = bf16[128,2048]{1,0:T(8,128)(2,1)S(1)} fusion(bf16[4096,2048]{1,0:T(8,128)(2,1)} %all-gather.11.cloned.1.call-done, bf16[128,4096]{1,0:T(8,128)(2,1)S(1)} %copy-done, f32[128]{0:T(128)S(1)} %add_rsqrt_fusion.1), kind=kOutput, calls=%fused_computation.19 | convolution fusion | flops 2149318656 | bytes 18350592 | tf_op jit(solution)/shard_map/dot_general | solution.py:63
  353.4 1.0 copy.51
  354.4 4.5 fusion.137
  358.9 2.7 fusion.15
  361.6 1.8 fusion.139
  363.4 0.5 fusion.22
  363.9 0.2 copy-done.2
  364.2 0.8 fusion.3
  365.0 1.3 fusion.21
  366.3 1.8 fusion.138
  368.2 0.1 fusion.136
  368.3 0.8 fusion.135
  369.0 1.3 collective-permute-start.3
  370.3 1.3 collective-permute-start.5
  371.6 1.3 collective-permute-start.4
  372.9 1.3 collective-permute-start.6
  374.2 1.5 collective-permute-start.8
  375.7 11.7 %fusion.141 = f32[128,4096]{1,0:T(8,128)S(1)} fusion(bf16[128,2048]{0,1:T(8,128)(2,1)} %bitcast.87, bf16[4096,2048]{1,0:T(8,128)(2,1)} %all-gather.11.cloned.1.call-done), kind=kOutput, calls=%fused_computation.182 | convolution fusion | flops 2147483648 | bytes 19398656 | tf_op jit(solution)/shard_map/tc,dc->td/dot_general | solution.py:141
  387.4 1.3 collective-permute-start.7
  388.8 1.2 fusion.91
  390.0 7.9 %collective-permute-done.7 = bf16[128,4,128]{0,2,1:T(8,128)(2,1)S(1)} collective-permute-done((bf16[128,4,128]{0,2,1:T(8,128)(2,1)S(1)}, bf16[128,4,128]{0,2,1:T(8,128)(2,1)S(1)}, u32[]{:S(2)}, u32[]{:S(2)}) %collective-permute-start.7) | collective-permute-done | bytes 131104 | tf_op jit(solution)/shard_map/ppermute | solution.py:14
  397.9 1.1 fusion.88
  399.0 7.3 %fusion.1 = bf16[128,4096]{1,0:T(8,128)(2,1)} fusion(f32[128,4096]{1,0:T(8,128)S(1)} %fusion.141, bf16[4096,1024]{1,0:T(8,128)(2,1)} %bitcast.80, bf16[128,512]{0,1:T(8,128)(2,1)S(1)} %bitcast.93, bf16[128,512]{0,1:T(8,128)(2,1)S(1)} %bitcast.92), kind=kOutput, calls=%fused_computation.2 | convolution fusion | flops 1075314688 | bytes 11796480 | tf_op jit(solution)/shard_map/tc,dc->td/dot_general | solution.py:142
  406.3 0.0 reduce-scatter.2.cloned.1.call-start
  406.3 40.4 %all-reduce.6.cloned.1.call-done = bf16[128,4096]{1,0:T(8,128)(2,1)} async-done(((bf16[128,4096]{1,0:T(8,128)(2,1)}), bf16[128,4096]{1,0:T(8,128)(2,1)}) %all-reduce.6.cloned.1.call-update) | async-done | bytes 1048592 | tf_op jit(solution)/shard_map/psum | solution.py:145
  446.8 1.8 fusion.9
  448.6 12.3 %convolution_convert_fusion.1 = bf16[128,2560]{1,0:T(8,128)(2,1)S(1)} fusion(bf16[2560,1280]{1,0:T(8,128)(2,1)} %bitcast.83, bf16[1280,4096]{1,0:T(8,128)(2,1)} %all-gather.7.cloned.1.call-done, bf16[128,4096]{1,0:T(8,128)(2,1)S(1)} %copy-done, bf16[128,4096]{1,0:T(8,128)(2,1)S(1)} %copy-done.5, f32[128]{0:T(128)S(1)} %broadcast_multiply_fusion.3, ...), kind=kOutput, calls=%fused_computation.9 | convolution fusion | flops 2186674176 | bytes 20448256 | tf_op jit(solution)/shard_map/th,fh->tf/dot_general | solution.py:150
  460.9 1.2 convert_element_type.119
  462.1 0.1 dynamic-slice.1
  462.2 16.2 %reduce-scatter.2.cloned.1.call-done = bf16[256,640]{1,0:T(8,128)(2,1)} async-done(((bf16[512,640]{1,0:T(8,128)(2,1)}), bf16[256,640]{1,0:T(8,128)(2,1)}) %reduce-scatter.2.cloned.1.call-update) | async-done | bytes 327696 | tf_op jit(solution)/shard_map/reduce_scatter | solution.py:153
  478.4 1.2 convert_reduce_fusion.1
  479.5 1.9 fusion.35
  (40 shorter events, 0.3 us)
Async XLA Ops:
  6.5 53.0 %all-gather.5.cloned.1.call-start = ((), (), s32[]{:S(2)}) async-start(), calls=%async_computation.1 | async-start | bytes 8192000 | tf_op jit(solution)/shard_map/all_gather | solution.py:45
  7.3 1.5 copy-start.3
  7.3 124.0 %all-gather.7.cloned.1.call-start = ((), (), s32[]{:S(2)}) async-start(), calls=%async_computation.2 | async-start | bytes 13107200 | tf_op jit(solution)/shard_map/all_gather | solution.py:49
  8.0 183.1 %all-gather.9.cloned.1.call-start = ((), (), s32[]{:S(2)}) async-start(), calls=%async_computation.4 | async-start | bytes 10485760 | tf_op jit(solution)/shard_map/all_gather | solution.py:58
  8.8 224.7 %all-reduce.4.cloned.1.call-start = ((), (), s32[]{:S(2)}) async-start(), calls=%async_computation.3 | async-start | bytes 2097152 | tf_op jit(solution)/shard_map/psum | solution.py:52
  63.4 75.7 %copy-start.6 = (f32[128,1280]{1,0:T(8,128)}, f32[128,1280]{1,0:T(8,128)S(1)}, u32[]{:S(2)}) copy-start(f32[128,1280]{1,0:T(8,128)S(1)} %fusion.140) | copy-start | bytes 1966084
  139.1 0.7 copy-start.9
  139.1 206.1 %all-gather.11.cloned.1.call-start = ((), (), s32[]{:S(2)}) async-start(), calls=%async_computation.5 | async-start | bytes 20971520 | tf_op jit(solution)/shard_map/all_gather | solution.py:57
  139.7 307.1 %all-reduce.6.cloned.1.call-start = ((), (), s32[]{:S(2)}) async-start(), calls=%async_computation.6 | async-start | bytes 2097152 | tf_op jit(solution)/shard_map/psum | solution.py:145
  235.0 11.9 %copy-start.8 = (bf16[128,2048]{1,0:T(8,128)(2,1)S(1)}, bf16[128,2048]{1,0:T(8,128)(2,1)}, u32[]{:S(2)}) copy-start(bf16[128,2048]{1,0:T(8,128)(2,1)} %param.12) | copy-start | bytes 1572868
  240.1 7.3 %collective-permute-start.2 = (bf16[128,1024]{1,0:T(8,128)(2,1)S(1)}, bf16[128,1024]{1,0:T(8,128)(2,1)S(1)}, u32[]{:S(2)}, u32[]{:S(2)}) collective-permute-start(bf16[128,1024]{1,0:T(8,128)(2,1)S(1)} %convolution_convert_fusion.3), channel_id=1, source_target_pairs={{0,2},{2,4},{4,6},{1,3},{3,5},{5,7},{8,10},{10,12},{12,14},{9,11},... | collective-permute-start | bytes 786440 | tf_op jit(solution)/shard_map/ppermute | solution.py:14
  241.7 15.8 %collective-permute-start.1 = (bf16[128,1024]{1,0:T(8,128)(2,1)S(1)}, bf16[128,1024]{1,0:T(8,128)(2,1)S(1)}, u32[]{:S(2)}, u32[]{:S(2)}) collective-permute-start(bf16[128,1024]{1,0:T(8,128)(2,1)S(1)} %convolution_convert_fusion.3), channel_id=1, source_target_pairs={{0,4},{2,6},{1,5},{3,7},{8,12},{10,14},{9,13},{11,15},{16,20},{18,... | collective-permute-start | bytes 786440 | tf_op jit(solution)/shard_map/ppermute | solution.py:14
  245.4 20.8 %collective-permute-start = (bf16[128,1024]{1,0:T(8,128)(2,1)S(1)}, bf16[128,1024]{1,0:T(8,128)(2,1)S(1)}, u32[]{:S(2)}, u32[]{:S(2)}) collective-permute-start(bf16[128,1024]{1,0:T(8,128)(2,1)S(1)} %convolution_convert_fusion.3), channel_id=1, source_target_pairs={{0,6},{1,7},{8,14},{9,15},{16,22},{17,23},{24,30},{25,31}} | collective-permute-start | bytes 786440 | tf_op jit(solution)/shard_map/ppermute | solution.py:14
  266.4 78.8 %copy-start = (bf16[128,4096]{1,0:T(8,128)(2,1)S(1)}, bf16[128,4096]{1,0:T(8,128)(2,1)}, u32[]{:S(2)}) copy-start(bf16[128,4096]{1,0:T(8,128)(2,1)} %all-reduce.4.cloned.1.call-done) | copy-start | bytes 3145732
  361.6 2.6 copy-start.2
  365.0 1.3 copy-start.4
  369.0 18.4 %collective-permute-start.3 = (bf16[128,4,128]{0,2,1:T(8,128)(2,1)}, bf16[128,4,128]{0,2,1:T(8,128)(2,1)}, u32[]{:S(2)}, u32[]{:S(2)}) collective-permute-start(bf16[128,4,128]{0,2,1:T(8,128)(2,1)} %get-tuple-element.13), channel_id=1, source_target_pairs={{2,0},{4,2},{6,4},{3,1},{5,3},{7,5},{10,8},{12,10},{14,12},{11,9},... | collective-permute-start | bytes 393224 | tf_op jit(solution)/shard_map/ppermute | solution.py:14
  370.3 18.4 %collective-permute-start.5 = (bf16[128,4,128]{0,2,1:T(8,128)(2,1)}, bf16[128,4,128]{0,2,1:T(8,128)(2,1)}, u32[]{:S(2)}, u32[]{:S(2)}) collective-permute-start(bf16[128,4,128]{0,2,1:T(8,128)(2,1)} %get-tuple-element.14), channel_id=1, source_target_pairs={{6,0},{7,1},{14,8},{15,9},{22,16},{23,17},{30,24},{31,25}} | collective-permute-start | bytes 393224 | tf_op jit(solution)/shard_map/ppermute | solution.py:14
  371.6 17.1 %collective-permute-start.4 = (bf16[128,4,128]{0,2,1:T(8,128)(2,1)}, bf16[128,4,128]{0,2,1:T(8,128)(2,1)}, u32[]{:S(2)}, u32[]{:S(2)}) collective-permute-start(bf16[128,4,128]{0,2,1:T(8,128)(2,1)} %get-tuple-element.15), channel_id=1, source_target_pairs={{4,0},{6,2},{5,1},{7,3},{12,8},{14,10},{13,9},{15,11},{20,16},{22,... | collective-permute-start | bytes 393224 | tf_op jit(solution)/shard_map/ppermute | solution.py:14
  372.9 17.0 %collective-permute-start.6 = (bf16[128,4,128]{0,2,1:T(8,128)(2,1)S(1)}, bf16[128,4,128]{0,2,1:T(8,128)(2,1)}, u32[]{:S(2)}, u32[]{:S(2)}) collective-permute-start(bf16[128,4,128]{0,2,1:T(8,128)(2,1)S(1)} %get-tuple-element.16), channel_id=1, source_target_pairs={{2,0},{4,2},{6,4},{3,1},{5,3},{7,5},{10,8},{12,10},{14,12},{11,9},... | collective-permute-start | bytes 393224 | tf_op jit(solution)/shard_map/ppermute | solution.py:14
  374.2 15.7 %collective-permute-start.8 = (bf16[128,4,128]{0,2,1:T(8,128)(2,1)S(1)}, bf16[128,4,128]{0,2,1:T(8,128)(2,1)}, u32[]{:S(2)}, u32[]{:S(2)}) collective-permute-start(bf16[128,4,128]{0,2,1:T(8,128)(2,1)S(1)} %get-tuple-element.17), channel_id=1, source_target_pairs={{6,0},{7,1},{14,8},{15,9},{22,16},{23,17},{30,24},{31,25}} | collective-permute-start | bytes 393224 | tf_op jit(solution)/shard_map/ppermute | solution.py:14
  387.4 10.4 %collective-permute-start.7 = (bf16[128,4,128]{0,2,1:T(8,128)(2,1)S(1)}, bf16[128,4,128]{0,2,1:T(8,128)(2,1)S(1)}, u32[]{:S(2)}, u32[]{:S(2)}) collective-permute-start(bf16[128,4,128]{0,2,1:T(8,128)(2,1)S(1)} %get-tuple-element.18), channel_id=1, source_target_pairs={{4,0},{6,2},{5,1},{7,3},{12,8},{14,10},{13,9},{15,11},{20,16},{22,... | collective-permute-start | bytes 393224 | tf_op jit(solution)/shard_map/ppermute | solution.py:14
  406.2 42.3 %copy-start.7 = (f32[128,1280]{1,0:T(8,128)S(1)}, f32[128,1280]{1,0:T(8,128)}, u32[]{:S(2)}) copy-start(f32[128,1280]{1,0:T(8,128)} %copy-done.6) | copy-start | bytes 1966084
  406.3 72.1 %reduce-scatter.2.cloned.1.call-start = ((), (), s32[]{:S(2)}) async-start(), calls=%async_computation.7 | async-start | bytes 983040 | tf_op jit(solution)/shard_map/reduce_scatter | solution.py:153
  446.8 1.8 copy-start.5
  460.9 17.5 %copy-start.1 = (f32[512,640]{1,0:T(8,128)S(1)}, f32[512,640]{1,0:T(8,128)}, u32[]{:S(2)}) copy-start(f32[512,640]{1,0:T(8,128)} %get-tuple-element.11) | copy-start | bytes 3932164
Sparse Core Ops, SparseCore 0:
  8.9 50.5 all-gather.4
  61.1 70.1 all-gather.6
  132.8 58.2 all-gather.8
  193.3 40.1 all-reduce.3
  234.9 110.2 all-gather.10
  406.4 40.3 all-reduce.5
  462.3 16.0 reduce-scatter.1
where the time goes:
time: 489 us; the launch traced here: 488 us
  waiting for transfers between devices  365 us (75%)
  matrix products  66.9 us (14%)
  starting transfers between devices  15 us (3%)
  local copies, waits for them, and re-layouts  14.4 us (3%)
  between operations  13.9 us (3%)
  other arithmetic  13.4 us (3%)
    all_gather x1, waiting for transfers between devices, local(): lax.all_gather(w_query, 'seq', axis=0, tiled=True)  77.9 us
    all_gather x1, waiting for transfers between devices, local(): second_tile = lax.all_gather(w_merge2, 'seq', axis=1, tiled=True)  67.9 us
    all_gather x1, waiting for transfers between devices, local(): lax.all_gather(w_keyval, 'seq', axis=0, tiled=True)  51.3 us
    all_gather x1, waiting for transfers between devices, local(): first_tile = lax.all_gather(w_merge1, 'seq', axis=1, tiled=True)  48.7 us
    psum x1, waiting for transfers between devices, local(): lax.psum(dnormed_part.astype(jnp.bfloat16), 'mp').astype(jnp.float32)  40.4 us
    psum x1, waiting for transfers between devices, local(): merged = lax.psum(partial_value.astype(jnp.bfloat16), 'mp')  33 us
    ppermute x9, waiting for transfers between devices, shifted_2(): lax.ppermute(value, axis, [(source, source + steps) for source in range(i...  26.7 us
    reduce_scatter x1, waiting for transfers between devices, local(): lax.psum_scatter(dmerge_part.reshape(patch_rows, feat_width).astype(jnp.b...  16.2 us
  transfers between devices with their start and end apart: 16, of which 10 were waited for; matrix products, arithmetic and copies ran while one was open for 9% of the time, Pallas kernels for 0%

commit v1 on v0

--- a/solution.py
+++ b/solution.py
@@ -2,10 +2,24 @@
 import jax.numpy as jnp
 from jax import lax
 from jax.sharding import PartitionSpec as P
+from jax.lax import all_to_all, axis_size
 
 HEAD = 128
 EPSILON = 1e-06
 NEGATIVE = 1e30
+
+
+def extend_ways(local_block):
+    upper = jnp.concatenate(
+        all_to_all(
+            jnp.stack([local_block for _ in range(axis_size("seq"))], axis=0),
+            "seq",
+            split_axis=0,
+            concat_axis=0,
+        ),
+        axis=1,
+    )
+    return upper
 
 
 def shifted_2(value, axis, steps):
@@ -46,7 +60,7 @@
     first_flat = first_tile.reshape(4 * feat_width, first_tile.shape[2])
     hidden_pre = jnp.dot(merge_in, first_flat, preferred_element_type=jnp.float32)
     hidden = jax.nn.gelu(hidden_pre, approximate=False).astype(jnp.bfloat16)
-    second_tile = lax.all_gather(w_merge2, "seq", axis=1, tiled=True)
+    second_tile = extend_ways(w_merge2)
     model_width = second_tile.shape[1]
     partial_value = jnp.dot(hidden, second_tile, preferred_element_type=jnp.float32)
     merged = lax.psum(partial_value.astype(jnp.bfloat16), "mp")

time: 489 us -> 537 us (1.098)
  waiting for transfers between devices: 365 us -> 399 us
  local copies, waits for them, and re-layouts: 14.4 us -> 23.2 us
    all_to_all x0 -> x1, waiting for transfers between devices: none -> 74.4 us  [extend_ways(): all_to_all(jnp.stack([local_block for _ in range(axis_size('seq'))], axis...]
    all_gather x1 -> x0, waiting for transfers between devices: 67.9 us -> none  [local(): second_tile = lax.all_gather(w_merge2, 'seq', axis=1, tiled=True)]
    all_gather x1, waiting for transfers between devices: 48.7 us -> 68.6 us  [local(): first_tile = lax.all_gather(w_merge1, 'seq', axis=1, tiled=True)]
    all_gather x1, waiting for transfers between devices: 77.9 us -> 70.3 us  [local(): lax.all_gather(w_query, 'seq', axis=0, tiled=True)]
    all_gather x1, waiting for transfers between devices: 51.3 us -> 58.3 us  [local(): lax.all_gather(w_keyval, 'seq', axis=0, tiled=True)]
    all_to_all x0 -> x1, starting transfers between devices: none -> 6.42 us  [extend_ways(): all_to_all(jnp.stack([local_block for _ in range(axis_size('seq'))], axis...]
    psum x1, waiting for transfers between devices: 33 us -> 38.8 us  [local(): merged = lax.psum(partial_value.astype(jnp.bfloat16), 'mp')]
    unnamed x23 -> x24, local copies, waits for them, and re-layouts: 10 us -> 14.1 us
where the time goes in v1:
time: 537 us; the launch traced here: 536 us
  waiting for transfers between devices  399 us (74%)
  matrix products  67 us (12%)
  local copies, waits for them, and re-layouts  23.2 us (4%)
  starting transfers between devices  19.7 us (4%)
  between operations  13.9 us (3%)
  other arithmetic  13.4 us (2%)
    all_to_all x1, waiting for transfers between devices, extend_ways(): all_to_all(jnp.stack([local_block for _ in range(axis_size('seq'))], axis...  74.4 us
    all_gather x1, waiting for transfers between devices, local(): lax.all_gather(w_query, 'seq', axis=0, tiled=True)  70.3 us
    all_gather x1, waiting for transfers between devices, local(): first_tile = lax.all_gather(w_merge1, 'seq', axis=1, tiled=True)  68.6 us
    all_gather x1, waiting for transfers between devices, local(): lax.all_gather(w_keyval, 'seq', axis=0, tiled=True)  58.3 us
    psum x1, waiting for transfers between devices, local(): lax.psum(dnormed_part.astype(jnp.bfloat16), 'mp').astype(jnp.float32)  41.6 us
    psum x1, waiting for transfers between devices, local(): merged = lax.psum(partial_value.astype(jnp.bfloat16), 'mp')  38.8 us
    ppermute x9, waiting for transfers between devices, shifted_2(): lax.ppermute(value, axis, [(source, source + steps) for source in range(i...  28.7 us
    reduce_scatter x1, waiting for transfers between devices, local(): lax.psum_scatter(dmerge_part.reshape(patch_rows, feat_width).astype(jnp.b...  16.2 us
  transfers between devices with their start and end apart: 16, of which 10 were waited for; matrix products, arithmetic and copies ran while one was open for 9% of the time, Pallas kernels for 0%

profile of v1, /device:TPU:0, one launch (start us, length us, event | category | flops | bytes accessed | tf_op | source)
XLA Modules:
  0.0 535.8 jit_solution(3851465798084823030)
XLA Ops:
  6.5 0.7 all-gather.4.cloned.1.call-update
  7.3 3.0 copy.33
  10.2 4.7 stack.2
  14.9 6.4 %all-to-all-start = ((bf16[4,1280,1024]{1,2,0:T(8,128)(2,1)}), bf16[4,1280,1024]{1,2,0:T(8,128)(2,1)}, u32[]{:S(2)}, u32[]{:S(2)}) async-start(bf16[4,1280,1024]{1,2,0:T(8,128)(2,1)} %stack.2), calls=%async_computation | async-start | bytes 20971520 | tf_op jit(solution)/shard_map/all_to_all | solution.py:14
  21.4 0.3 convert_reduce_fusion
  21.7 1.3 fusion.20
  23.0 0.4 reshape.117
  23.4 68.6 %all-gather.4.cloned.1.call-done = bf16[4,640,1280]{2,1,0:T(8,128)(2,1)} async-done(((bf16[4,160,1280]{2,1,0:T(8,128)(2,1)}), bf16[4,640,1280]{2,1,0:T(8,128)(2,1)}) %all-gather.4.cloned.1.call-update) | async-done | bytes 6553616 | tf_op jit(solution)/shard_map/all_gather | solution.py:59
  92.0 3.9 fusion.140
  95.9 74.4 %all-to-all-done = bf16[4,1280,1024]{1,2,0:T(8,128)(2,1)} async-done(((bf16[4,1280,1024]{1,2,0:T(8,128)(2,1)}), bf16[4,1280,1024]{1,2,0:T(8,128)(2,1)}, u32[]{:S(2)}, u32[]{:S(2)}) %all-to-all-start) | async-done | bytes 10485792 | tf_op jit(solution)/shard_map/all_to_all | solution.py:14
  170.2 9.4 %convolution_convert_fusion = bf16[128,4096]{1,0:T(8,128)(2,1)} fusion(bf16[1280,4096]{0,1:T(8,128)(2,1)} %bitcast.2, f32[128,1280]{1,0:T(8,128)S(1)} %fusion.140), kind=kOutput, calls=%fused_computation.3 | convolution fusion | flops 1353351168 | bytes 12189696 | tf_op jit(solution)/shard_map/dot_general | solution.py:65
  179.7 0.7 all-gather.6.cloned.1.call-update
  180.4 0.5 all-gather.8.cloned.1.call-update
  181.1 0.1 pad_dynamic-slice_fusion
  181.1 38.8 %all-reduce.4.cloned.1.call-done = bf16[128,4096]{1,0:T(8,128)(2,1)} async-done(((bf16[128,4096]{1,0:T(8,128)(2,1)}), bf16[128,4096]{1,0:T(8,128)(2,1)}) %all-reduce.4.cloned.1.call-update) | async-done | bytes 1048592 | tf_op jit(solution)/shard_map/psum | solution.py:66
  219.9 1.5 fusion.8
  221.4 58.3 %all-gather.6.cloned.1.call-done = bf16[4096,2,512]{2,1,0:T(2,128)(2,1)} async-done(((bf16[1024,2,512]{2,1,0:T(2,128)(2,1)}), bf16[4096,2,512]{2,1,0:T(2,128)(2,1)}) %all-gather.6.cloned.1.call-update) | async-done | bytes 8388624 | tf_op jit(solution)/shard_map/all_gather | solution.py:72
  279.8 10.4 %copy.66 = bf16[512,8,2,512]{3,1,2,0:T(8,128)(2,1)} copy(bf16[512,8,2,512]{3,2,1,0:T(2,128)(2,1)} %bitcast.84) | data formatting | bytes 16777216
  290.2 6.2 %convolution_convert_fusion.3 = bf16[128,1024]{1,0:T(8,128)(2,1)S(1)} fusion(bf16[4096,1024]{1,0:T(8,128)(2,1)} %bitcast.82, bf16[128,4096]{1,0:T(8,128)(2,1)S(1)} %copy-done, f32[128]{0:T(128)S(1)} %add_rsqrt_fusion.1), kind=kOutput, calls=%fused_computation.43 | convolution fusion | flops 1075445760 | bytes 9699840 | tf_op jit(solution)/shard_map/dot_general | solution.py:80
  296.4 2.1 collective-permute-start.2
  298.5 1.5 collective-permute-start.1
  300.0 1.5 collective-permute-start
  301.5 0.3 copy.36
  301.8 0.2 compare_and_fusion
  302.0 10.2 %collective-permute-done.1 = bf16[128,1024]{1,0:T(8,128)(2,1)S(1)} collective-permute-done((bf16[128,1024]{1,0:T(8,128)(2,1)S(1)}, bf16[128,1024]{1,0:T(8,128)(2,1)S(1)}, u32[]{:S(2)}, u32[]{:S(2)}) %collective-permute-start.1) | collective-permute-done | bytes 262176 | tf_op jit(solution)/shard_map/ppermute | solution.py:28
  312.3 10.6 %collective-permute-done = bf16[128,1024]{1,0:T(8,128)(2,1)S(1)} collective-permute-done((bf16[128,1024]{1,0:T(8,128)(2,1)S(1)}, bf16[128,1024]{1,0:T(8,128)(2,1)S(1)}, u32[]{:S(2)}, u32[]{:S(2)}) %collective-permute-start) | collective-permute-done | bytes 262176 | tf_op jit(solution)/shard_map/ppermute | solution.py:28
  322.9 0.1 pad_maximum_fusion
  322.9 0.1 fusion.134
  323.0 0.1 reshape.124
  323.1 0.3 copy.49
  323.5 0.1 reshape.122
  323.6 0.3 copy.51
  323.9 70.3 %all-gather.8.cloned.1.call-done = bf16[4096,2048]{1,0:T(8,128)(2,1)} async-done(((bf16[1024,2048]{1,0:T(8,128)(2,1)}), bf16[4096,2048]{1,0:T(8,128)(2,1)}) %all-gather.8.cloned.1.call-update) | async-done | bytes 16777232 | tf_op jit(solution)/shard_map/all_gather | solution.py:71
  394.2 8.1 %convolution_convert_fusion.2 = bf16[128,2048]{1,0:T(8,128)(2,1)S(1)} fusion(bf16[4096,2048]{1,0:T(8,128)(2,1)} %all-gather.8.cloned.1.call-done, bf16[128,4096]{1,0:T(8,128)(2,1)S(1)} %copy-done, f32[128]{0:T(128)S(1)} %add_rsqrt_fusion.1), kind=kOutput, calls=%fused_computation.19 | convolution fusion | flops 2149318656 | bytes 18350592 | tf_op jit(solution)/shard_map/dot_general | solution.py:77
  402.3 1.0 copy.65
  403.4 4.5 fusion.137
  407.9 2.7 fusion.15
  410.6 1.8 fusion.139
  412.4 0.5 fusion.22
  412.9 0.2 copy-done.2
  413.1 0.8 fusion.3
  414.0 1.3 fusion.21
  415.3 1.8 fusion.138
  417.1 0.1 fusion.136
  417.2 0.8 fusion.135
  418.0 1.3 collective-permute-start.3
  419.3 1.3 collective-permute-start.5
  420.6 1.3 collective-permute-start.4
  421.9 1.3 collective-permute-start.6
  423.2 1.5 collective-permute-start.8
  424.7 11.7 %fusion.141 = f32[128,4096]{1,0:T(8,128)S(1)} fusion(bf16[128,2048]{0,1:T(8,128)(2,1)} %bitcast.90, bf16[4096,2048]{1,0:T(8,128)(2,1)} %all-gather.8.cloned.1.call-done), kind=kOutput, calls=%fused_computation.182 | convolution fusion | flops 2147483648 | bytes 19398656 | tf_op jit(solution)/shard_map/tc,dc->td/dot_general | solution.py:155
  436.4 1.3 collective-permute-start.7
  437.7 1.2 fusion.91
  438.9 7.9 %collective-permute-done.7 = bf16[128,4,128]{0,2,1:T(8,128)(2,1)S(1)} collective-permute-done((bf16[128,4,128]{0,2,1:T(8,128)(2,1)S(1)}, bf16[128,4,128]{0,2,1:T(8,128)(2,1)S(1)}, u32[]{:S(2)}, u32[]{:S(2)}) %collective-permute-start.7) | collective-permute-done | bytes 131104 | tf_op jit(solution)/shard_map/ppermute | solution.py:28
  446.8 1.1 fusion.88
  448.0 7.3 %fusion.1 = bf16[128,4096]{1,0:T(8,128)(2,1)} fusion(f32[128,4096]{1,0:T(8,128)S(1)} %fusion.141, bf16[4096,1024]{1,0:T(8,128)(2,1)} %bitcast.83, bf16[128,512]{0,1:T(8,128)(2,1)S(1)} %bitcast.96, bf16[128,512]{0,1:T(8,128)(2,1)S(1)} %bitcast.95), kind=kOutput, calls=%fused_computation.2 | convolution fusion | flops 1075314688 | bytes 11796480 | tf_op jit(solution)/shard_map/tc,dc->td/dot_general | solution.py:156
  455.3 41.6 %all-reduce.6.cloned.1.call-done = bf16[128,4096]{1,0:T(8,128)(2,1)} async-done(((bf16[128,4096]{1,0:T(8,128)(2,1)}), bf16[128,4096]{1,0:T(8,128)(2,1)}) %all-reduce.6.cloned.1.call-update) | async-done | bytes 1048592 | tf_op jit(solution)/shard_map/psum | solution.py:159
  496.9 1.8 fusion.9
  498.7 9.7 %convolution_convert_fusion.1 = bf16[128,2560]{1,0:T(8,128)(2,1)S(1)} fusion(bf16[2560,1280]{1,0:T(8,128)(2,1)} %bitcast.86, bf16[1280,4096]{0,1:T(8,128)(2,1)} %bitcast.2, bf16[128,4096]{1,0:T(8,128)(2,1)S(1)} %copy-done, bf16[128,4096]{1,0:T(8,128)(2,1)S(1)} %copy-done.5, f32[128]{0:T(128)S(1)} %broadcast_multiply_fusion.3, f32[128]{0:T(128)S(1)} %add_rsqrt_fusion.1, ...), kind=kOutput, calls=%fused_computation.9 | convolution fusion | flops 2186674176 | bytes 20448256 | tf_op jit(solution)/shard_map/th,fh->tf/dot_general | solution.py:164
  508.4 1.2 convert_element_type.119
  509.7 0.1 dynamic-slice.1
  509.7 16.2 %reduce-scatter.2.cloned.1.call-done = bf16[256,640]{1,0:T(8,128)(2,1)} async-done(((bf16[512,640]{1,0:T(8,128)(2,1)}), bf16[256,640]{1,0:T(8,128)(2,1)}) %reduce-scatter.2.cloned.1.call-update) | async-done | bytes 327696 | tf_op jit(solution)/shard_map/reduce_scatter | solution.py:167
  525.9 1.2 convert_reduce_fusion.1
  527.1 1.9 fusion.35
  (41 shorter events, 0.4 us)
Async XLA Ops:
  6.5 85.5 %all-gather.4.cloned.1.call-start = ((), (), s32[]{:S(2)}) async-start(), calls=%async_computation.2 | async-start | bytes 8192000 | tf_op jit(solution)/shard_map/all_gather | solution.py:59
  14.9 6.5 %copy-start.3 = (bf16[512,640]{1,0:T(8,128)(2,1)S(1)}, bf16[512,640]{1,0:T(8,128)(2,1)}, u32[]{:S(2)}) copy-start(bf16[512,640]{1,0:T(8,128)(2,1)} %param.7) | copy-start | bytes 1966084
  14.9 155.3 %all-to-all-start = ((bf16[4,1280,1024]{1,2,0:T(8,128)(2,1)}), bf16[4,1280,1024]{1,2,0:T(8,128)(2,1)}, u32[]{:S(2)}, u32[]{:S(2)}) async-start(bf16[4,1280,1024]{1,2,0:T(8,128)(2,1)} %stack.2), calls=%async_computation | async-start | bytes 20971520 | tf_op jit(solution)/shard_map/all_to_all | solution.py:14
  21.3 198.5 %all-reduce.4.cloned.1.call-start = ((), (), s32[]{:S(2)}) async-start(), calls=%async_computation.3 | async-start | bytes 2097152 | tf_op jit(solution)/shard_map/psum | solution.py:66
  95.9 83.7 %copy-start.6 = (f32[128,1280]{1,0:T(8,128)}, f32[128,1280]{1,0:T(8,128)S(1)}, u32[]{:S(2)}) copy-start(f32[128,1280]{1,0:T(8,128)S(1)} %fusion.140) | copy-start | bytes 1966084
  179.6 100.1 %all-gather.6.cloned.1.call-start = ((), (), s32[]{:S(2)}) async-start(), calls=%async_computation.4 | async-start | bytes 10485760 | tf_op jit(solution)/shard_map/all_gather | solution.py:72
  180.4 0.7 copy-start.9
  180.4 213.8 %all-gather.8.cloned.1.call-start = ((), (), s32[]{:S(2)}) async-start(), calls=%async_computation.5 | async-start | bytes 20971520 | tf_op jit(solution)/shard_map/all_gather | solution.py:71
  181.0 315.9 %all-reduce.6.cloned.1.call-start = ((), (), s32[]{:S(2)}) async-start(), calls=%async_computation.6 | async-start | bytes 2097152 | tf_op jit(solution)/shard_map/psum | solution.py:159
  279.8 10.4 %copy-start = (bf16[128,4096]{1,0:T(8,128)(2,1)S(1)}, bf16[128,4096]{1,0:T(8,128)(2,1)}, u32[]{:S(2)}) copy-start(bf16[128,4096]{1,0:T(8,128)(2,1)} %all-reduce.4.cloned.1.call-done) | copy-start | bytes 3145732
  290.2 11.3 %copy-start.8 = (bf16[128,2048]{1,0:T(8,128)(2,1)S(1)}, bf16[128,2048]{1,0:T(8,128)(2,1)}, u32[]{:S(2)}) copy-start(bf16[128,2048]{1,0:T(8,128)(2,1)} %param.12) | copy-start | bytes 1572868
  296.4 5.6 %collective-permute-start.2 = (bf16[128,1024]{1,0:T(8,128)(2,1)S(1)}, bf16[128,1024]{1,0:T(8,128)(2,1)S(1)}, u32[]{:S(2)}, u32[]{:S(2)}) collective-permute-start(bf16[128,1024]{1,0:T(8,128)(2,1)S(1)} %convolution_convert_fusion.3), channel_id=1, source_target_pairs={{0,2},{2,4},{4,6},{1,3},{3,5},{5,7},{8,10},{10,12},{12,14},{9,11},... | collective-permute-start | bytes 786440 | tf_op jit(solution)/shard_map/ppermute | solution.py:28
  298.5 13.8 %collective-permute-start.1 = (bf16[128,1024]{1,0:T(8,128)(2,1)S(1)}, bf16[128,1024]{1,0:T(8,128)(2,1)S(1)}, u32[]{:S(2)}, u32[]{:S(2)}) collective-permute-start(bf16[128,1024]{1,0:T(8,128)(2,1)S(1)} %convolution_convert_fusion.3), channel_id=1, source_target_pairs={{0,4},{2,6},{1,5},{3,7},{8,12},{10,14},{9,13},{11,15},{16,20},{18,... | collective-permute-start | bytes 786440 | tf_op jit(solution)/shard_map/ppermute | solution.py:28
  300.0 22.8 %collective-permute-start = (bf16[128,1024]{1,0:T(8,128)(2,1)S(1)}, bf16[128,1024]{1,0:T(8,128)(2,1)S(1)}, u32[]{:S(2)}, u32[]{:S(2)}) collective-permute-start(bf16[128,1024]{1,0:T(8,128)(2,1)S(1)} %convolution_convert_fusion.3), channel_id=1, source_target_pairs={{0,6},{1,7},{8,14},{9,15},{16,22},{17,23},{24,30},{25,31}} | collective-permute-start | bytes 786440 | tf_op jit(solution)/shard_map/ppermute | solution.py:28
  410.6 2.6 copy-start.2
  414.0 1.3 copy-start.4
  418.0 18.4 %collective-permute-start.3 = (bf16[128,4,128]{0,2,1:T(8,128)(2,1)}, bf16[128,4,128]{0,2,1:T(8,128)(2,1)}, u32[]{:S(2)}, u32[]{:S(2)}) collective-permute-start(bf16[128,4,128]{0,2,1:T(8,128)(2,1)} %get-tuple-element.13), channel_id=1, source_target_pairs={{2,0},{4,2},{6,4},{3,1},{5,3},{7,5},{10,8},{12,10},{14,12},{11,9},... | collective-permute-start | bytes 393224 | tf_op jit(solution)/shard_map/ppermute | solution.py:28
  419.3 18.4 %collective-permute-start.5 = (bf16[128,4,128]{0,2,1:T(8,128)(2,1)}, bf16[128,4,128]{0,2,1:T(8,128)(2,1)}, u32[]{:S(2)}, u32[]{:S(2)}) collective-permute-start(bf16[128,4,128]{0,2,1:T(8,128)(2,1)} %get-tuple-element.14), channel_id=1, source_target_pairs={{6,0},{7,1},{14,8},{15,9},{22,16},{23,17},{30,24},{31,25}} | collective-permute-start | bytes 393224 | tf_op jit(solution)/shard_map/ppermute | solution.py:28
  420.6 17.1 %collective-permute-start.4 = (bf16[128,4,128]{0,2,1:T(8,128)(2,1)}, bf16[128,4,128]{0,2,1:T(8,128)(2,1)}, u32[]{:S(2)}, u32[]{:S(2)}) collective-permute-start(bf16[128,4,128]{0,2,1:T(8,128)(2,1)} %get-tuple-element.15), channel_id=1, source_target_pairs={{4,0},{6,2},{5,1},{7,3},{12,8},{14,10},{13,9},{15,11},{20,16},{22,... | collective-permute-start | bytes 393224 | tf_op jit(solution)/shard_map/ppermute | solution.py:28
  421.9 17.0 %collective-permute-start.6 = (bf16[128,4,128]{0,2,1:T(8,128)(2,1)S(1)}, bf16[128,4,128]{0,2,1:T(8,128)(2,1)}, u32[]{:S(2)}, u32[]{:S(2)}) collective-permute-start(bf16[128,4,128]{0,2,1:T(8,128)(2,1)S(1)} %get-tuple-element.16), channel_id=1, source_target_pairs={{2,0},{4,2},{6,4},{3,1},{5,3},{7,5},{10,8},{12,10},{14,12},{11,9},... | collective-permute-start | bytes 393224 | tf_op jit(solution)/shard_map/ppermute | solution.py:28
  423.2 15.7 %collective-permute-start.8 = (bf16[128,4,128]{0,2,1:T(8,128)(2,1)S(1)}, bf16[128,4,128]{0,2,1:T(8,128)(2,1)}, u32[]{:S(2)}, u32[]{:S(2)}) collective-permute-start(bf16[128,4,128]{0,2,1:T(8,128)(2,1)S(1)} %get-tuple-element.17), channel_id=1, source_target_pairs={{6,0},{7,1},{14,8},{15,9},{22,16},{23,17},{30,24},{31,25}} | collective-permute-start | bytes 393224 | tf_op jit(solution)/shard_map/ppermute | solution.py:28
  436.4 10.4 %collective-permute-start.7 = (bf16[128,4,128]{0,2,1:T(8,128)(2,1)S(1)}, bf16[128,4,128]{0,2,1:T(8,128)(2,1)S(1)}, u32[]{:S(2)}, u32[]{:S(2)}) collective-permute-start(bf16[128,4,128]{0,2,1:T(8,128)(2,1)S(1)} %get-tuple-element.18), channel_id=1, source_target_pairs={{4,0},{6,2},{5,1},{7,3},{12,8},{14,10},{13,9},{15,11},{20,16},{22,... | collective-permute-start | bytes 393224 | tf_op jit(solution)/shard_map/ppermute | solution.py:28
  455.2 43.5 %copy-start.7 = (f32[128,1280]{1,0:T(8,128)S(1)}, f32[128,1280]{1,0:T(8,128)}, u32[]{:S(2)}) copy-start(f32[128,1280]{1,0:T(8,128)} %copy-done.6) | copy-start | bytes 1966084
  455.2 70.6 %reduce-scatter.2.cloned.1.call-start = ((), (), s32[]{:S(2)}) async-start(), calls=%async_computation.7 | async-start | bytes 983040 | tf_op jit(solution)/shard_map/reduce_scatter | solution.py:167
  496.9 1.8 copy-start.5
  508.4 17.5 %copy-start.1 = (f32[512,640]{1,0:T(8,128)S(1)}, f32[512,640]{1,0:T(8,128)}, u32[]{:S(2)}) copy-start(f32[512,640]{1,0:T(8,128)} %get-tuple-element.11) | copy-start | bytes 3932164
Sparse Core Ops, SparseCore 0:
  8.9 83.0 all-gather.3
  179.8 40.0 all-reduce.3
  221.5 58.2 all-gather.5
  281.2 112.9 all-gather.7
  455.4 41.4 all-reduce.5
  509.8 16.0 reduce-scatter.1
